TPU v7x, 256 devices: a whole 4x4x8 slice. The times are simulated.
256 devices in a mesh: bank: 16 (over z, core), zero: 16 (over y, x).
Axes of the slice: x: 4, y: 4, z: 8, core: 2. Of those that a mesh axis runs over, the one named last changes fastest.
Arguments:
- master_gate: float32 [64, 2048, 1408], P('bank', 'zero'), may hold values from -0.1875 to 0.1875
- master_up: float32 [64, 2048, 1408], P('bank', 'zero'), may hold values from -0.1875 to 0.1875
- master_down: float32 [64, 1408, 2048], P('bank', None, 'zero'), may hold values from -0.21875 to 0.21875
- router_weight: float32 [2048, 64], P('zero', 'bank'), may hold values from -0.125 to 0.125
- router_gain: float32 [2048], P('zero'), may hold values from 0.25 to 1.75
Outputs:
- final_gate: bfloat16 [64, 2048, 1408], P('bank', None, 'zero')
- final_up: bfloat16 [64, 2048, 1408], P('bank', None, 'zero')
- final_down: bfloat16 [64, 1408, 2048], P('bank', 'zero')
- scale_gate: float32 [64, 1408], P('bank', 'zero')
- scale_up: float32 [64, 1408], P('bank', 'zero')
- scale_down: float32 [64, 1408], P('bank', 'zero')
- serve_router: bfloat16 [2048, 64], replicated
All inputs are finite; a program needn't handle non-finite values. Where the computation divides by a largest or mean magnitude, that divisor is 1e-20 or more.
Results may differ from a plain program's by a relative error of at most 0.0013.
Values may be sent and summed in bfloat16 or wider, within the bound.
A program may use at most 64 MiB of HBM per device.

v0:
```python
import jax
import jax.numpy as jnp
from jax import lax
from jax.sharding import PartitionSpec as P

D_MODEL = 2048


def copy_for_each(x, axis):
    count = lax.axis_size(axis)
    return lax.all_to_all(jnp.broadcast_to(x[None], (count, *x.shape)), axis, 0, 0, tiled=True)


def taken_together(x, axis):
    return copy_for_each(x, axis).sum(axis=0)


def in_one(arrays, axis):
    vector, at, finished = (jnp.concatenate([a.reshape(-1) for a in arrays]), 0, [])
    total = taken_together(vector, axis)
    for a in arrays:
        finished.append(total[at : at + a.size].reshape(a.shape))
        at += a.size
    return tuple(finished)


def side_by_side(arrays, axis, split_dim, concat_dim, along):
    both = jnp.concatenate(arrays, axis=along)
    whole, at, finished = (
        lax.all_to_all(both, axis, split_axis=split_dim, concat_axis=concat_dim, tiled=True),
        0,
        [],
    )
    for a in arrays:
        finished.append(lax.slice_in_dim(whole, at, at + a.shape[along], axis=along))
        at += a.shape[along]
    return tuple(finished)


def laid_out(pieces, dim):
    shape = list(pieces.shape[1:])
    shape[dim] *= pieces.shape[0]
    return jnp.moveaxis(pieces, 0, dim).reshape(shape)


def gather_directly(x, axis, dim):
    pieces = copy_for_each(x, axis)
    return laid_out(pieces, dim)


def local(master_gate, master_up, master_down, router_weight, router_gain):
    total_gate, total_up, total_down = in_one(
        (
            jnp.sum(jnp.abs(master_gate), axis=1),
            jnp.sum(jnp.abs(master_up), axis=1),
            jnp.sum(jnp.abs(master_down), axis=2),
        ),
        "zero",
    )
    scale_gate = total_gate / D_MODEL
    scale_up = total_up / D_MODEL
    scale_down = total_down / D_MODEL
    narrow_gate, narrow_up, narrow_down = (
        (master_gate / jnp.expand_dims(scale_gate, 1)).astype(jnp.bfloat16),
        (master_up / jnp.expand_dims(scale_up, 1)).astype(jnp.bfloat16),
        (master_down / jnp.expand_dims(scale_down, 2)).astype(jnp.bfloat16),
    )
    final_gate, final_up = side_by_side((narrow_gate, narrow_up), "zero", 2, 1, 0)
    final_down = lax.all_to_all(narrow_down, "zero", split_axis=1, concat_axis=2, tiled=True)
    scale_gate = lax.dynamic_slice_in_dim(
        scale_gate, lax.axis_index("zero") * final_gate.shape[2], final_gate.shape[2], axis=1
    )
    scale_up = lax.dynamic_slice_in_dim(
        scale_up, lax.axis_index("zero") * final_up.shape[2], final_up.shape[2], axis=1
    )
    scale_down = lax.dynamic_slice_in_dim(
        scale_down, lax.axis_index("zero") * final_down.shape[1], final_down.shape[1], axis=1
    )
    part_router = (router_weight * router_gain[:, None]).astype(jnp.bfloat16)
    row_router = gather_directly(part_router, "zero", 0)
    serve_router = lax.all_gather(row_router, "bank", axis=1, tiled=True)
    return (final_gate, final_up, final_down, scale_gate, scale_up, scale_down, serve_router)


def solution(mesh):
    placed = (
        P("bank", "zero", None),
        P("bank", "zero", None),
        P("bank", None, "zero"),
        P("zero", "bank"),
        P("zero"),
    )
    return jax.shard_map(
        local,
        mesh=mesh,
        in_specs=placed,
        out_specs=(
            P("bank", None, "zero"),
            P("bank", None, "zero"),
            P("bank", "zero", None),
            P("bank", "zero"),
            P("bank", "zero"),
            P("bank", "zero"),
            P(),
        ),
        check_vma=False,
    )
```

profile of v0, /device:TPU:224, one launch (start us, length us, event | category | flops | bytes accessed | tf_op | source)
XLA Modules:
  0.0 125.6 jit_solution(8950060846199024515)
XLA Ops:
  0.6 0.0 copy-start.1
  0.6 2.2 %abs_reduce_fusion.2 = f32[4,1408]{1,0:T(4,128)S(1)} fusion(f32[4,128,1408]{2,1,0:T(8,128)} %param.5), kind=kLoop, calls=%fused_computation.4 | loop fusion | flops 1436160 | bytes 2906112 | tf_op jit(solution)/shard_map/reduce_sum | solution.py:54
  2.9 0.4 copy-done.1
  3.3 0.2 abs_reduce_fusion.1
  3.6 0.0 copy-start
  3.6 2.8 %abs_reduce_fusion = f32[4,1408]{1,0:T(4,128)S(1)} fusion(f32[4,1408,128]{2,1,0:T(8,128)} %param.7), kind=kLoop, calls=%fused_computation.2 | loop fusion | flops 1436160 | bytes 2906112 | tf_op jit(solution)/shard_map/reduce_sum | solution.py:56
  6.4 1.5 %broadcast_in_dim.4 = f32[16,1,16896]{2,1,0:T(1,128)} broadcast(f32[16896]{0:T(1024)S(1)} %pad_maximum_fusion.1), dimensions={2} | broadcast | bytes 1148928 | tf_op jit(solution)/shard_map/broadcast_in_dim | solution.py:11
  8.0 7.1 %all-to-all-start = ((f32[16,1,16896]{2,1,0:T(1,128)}), f32[16,1,16896]{2,1,0:T(1,128)}, u32[]{:S(2)}, u32[]{:S(2)}) async-start(f32[16,1,16896]{2,1,0:T(1,128)} %broadcast_in_dim.4), calls=%async_computation | async-start | bytes 2162688 | tf_op jit(solution)/shard_map/all_to_all | solution.py:11
  15.1 0.0 copy-done
  15.1 2.9 %copy.44 = f32[4,128,1408]{1,0,2:T(4,128)} copy(f32[4,128,1408]{2,1,0:T(8,128)S(1)} %copy-done) | data formatting | bytes 5767168 | tf_op args[0]
  17.9 0.0 copy-start.4
  17.9 0.0 copy-start.5
  17.9 0.0 copy-start.2
  17.9 4.6 %copy.46 = f32[4,128,1408]{1,0,2:T(4,128)} copy(f32[4,128,1408]{2,1,0:T(8,128)} %param.6) | data formatting | bytes 5767168 | tf_op args[1]
  22.6 0.0 copy-done.4
  22.6 0.0 copy-done.5
  22.6 10.6 %all-to-all-done = f32[16,1,16896]{2,1,0:T(1,128)} async-done(((f32[16,1,16896]{2,1,0:T(1,128)}), f32[16,1,16896]{2,1,0:T(1,128)}, u32[]{:S(2)}, u32[]{:S(2)}) %all-to-all-start) | async-done | bytes 1081376 | tf_op jit(solution)/shard_map/all_to_all | solution.py:11
  33.2 0.6 broadcast_in_dim.5
  33.8 3.5 %all-to-all-start.3 = ((bf16[16,128,4]{1,2,0:T(4,128)(2,1)}), bf16[16,128,4]{1,2,0:T(4,128)(2,1)S(1)}, u32[]{:S(2)}, u32[]{:S(2)}) async-start(bf16[16,128,4]{1,2,0:T(4,128)(2,1)} %broadcast_in_dim.5), calls=%async_computation.3 | async-start | bytes 32768 | tf_op jit(solution)/shard_map/all_to_all | solution.py:11
  37.3 1.9 %reduce_sum.39 = f32[16896]{0:T(1024)S(1)} reduce(f32[16,1,16896]{2,1,0:T(1,128)} %all-to-all-done, f32[]{:T(128)} %constant.6.clone.1), dimensions={0,1}, to_apply=%region_3.0 | reduce | flops 253440 | bytes 1148932 | tf_op jit(solution)/shard_map/reduce_sum | solution.py:15
  39.2 1.2 copy.50
  40.4 0.0 copy-done.2
  40.4 7.7 %fusion = bf16[4,1408,128]{2,0,1:T(4,128)(2,1)} fusion(f32[4,1408,128]{2,1,0:T(8,128)S(1)} %copy-done.2, f32[4,1408]{0,1:T(8,128)} %copy.50), kind=kLoop, calls=%fused_computation.5 | loop fusion | flops 1441792 | bytes 4347904 | tf_op jit(solution)/shard_map/convert_element_type | solution.py:66
  48.1 0.0 copy-start.3
  48.1 1.2 copy.43
  49.3 1.2 copy.45
  50.5 0.0 all-to-all-done.3
  50.5 7.2 %all-to-all-start.2 = ((bf16[4,1408,128]{2,0,1:T(4,128)(2,1)}), bf16[4,1408,128]{2,0,1:T(4,128)(2,1)}, u32[]{:S(2)}, u32[]{:S(2)}) async-start(bf16[4,1408,128]{2,0,1:T(4,128)(2,1)} %fusion), calls=%async_computation.2 | async-start | bytes 2883584 | tf_op jit(solution)/shard_map/all_to_all | solution.py:69
  57.7 0.0 copy-done.3
  57.7 6.6 %divide_convert_fusion = (bf16[4,128,1408]{1,0,2:T(4,128)(2,1)S(1)}, bf16[4,128,1408]{1,0,2:T(4,128)(2,1)S(1)}) fusion(f32[4,128,1408]{1,0,2:T(4,128)} %copy.46, f32[4,1408]{0,1:T(8,128)} %copy.45, f32[4,128,1408]{1,0,2:T(4,128)S(1)} %copy-done.3, f32[4,1408]{0,1:T(8,128)} %copy.43), kind=kLoop, calls=%fused_computation.6 | loop fusion | flops 2883584 | bytes 8695808 | tf_op jit(solution)/shard_map/convert_element_type | solution.py:65
  64.2 2.6 %pad_maximum_fusion = bf16[8,128,1408]{1,0,2:T(8,128)(2,1)} fusion(bf16[4,128,1408]{1,0,2:T(4,128)(2,1)S(1)} %get-tuple-element.12, bf16[4,128,1408]{1,0,2:T(4,128)(2,1)S(1)} %get-tuple-element.13), kind=kLoop, calls=%fused_computation | loop fusion | flops 5767168 | bytes 5767168 | tf_op jit(solution)/shard_map/concatenate | solution.py:28
  66.9 12.0 %all-to-all-done.2 = bf16[4,1408,128]{2,0,1:T(4,128)(2,1)} async-done(((bf16[4,1408,128]{2,0,1:T(4,128)(2,1)}), bf16[4,1408,128]{2,0,1:T(4,128)(2,1)}, u32[]{:S(2)}, u32[]{:S(2)}) %all-to-all-start.2) | async-done | bytes 1441824 | tf_op jit(solution)/shard_map/all_to_all | solution.py:69
  78.8 3.7 %all-to-all-start.1 = ((bf16[8,128,1408]{1,0,2:T(8,128)(2,1)}), bf16[8,128,1408]{1,0,2:T(8,128)(2,1)S(1)}, u32[]{:S(2)}, u32[]{:S(2)}) async-start(bf16[8,128,1408]{1,0,2:T(8,128)(2,1)} %pad_maximum_fusion), calls=%async_computation.1 | async-start | bytes 5767168 | tf_op jit(solution)/shard_map/all_to_all | solution.py:30
  82.6 14.6 %all-gather = bf16[16,4,2048]{2,1,0:T(4,128)(2,1)S(1)} all-gather(bf16[1,4,2048]{2,1,0:T(4,128)(2,1)S(1)} %bitcast.28), channel_id=1, replica_groups=mesh['bank'=16,'zero'=16] {'bank'}, dimensions={0}, use_global_device_ids=true | all-gather | bytes 278528 | tf_op jit(solution)/shard_map/all_gather | solution.py:81
  97.2 0.8 reshape.77
  98.0 0.6 constant_dynamic-slice_fusion.2
  98.6 0.7 constant_dynamic-slice_fusion
  99.3 3.0 %copy.52 = bf16[4,88,16,128]{3,2,1,0:T(8,128)(2,1)} copy(bf16[4,88,16,128]{3,0,1,2:T(4,128)(2,1)} %bitcast.4) | data formatting | bytes 2883584 | tf_op jit(solution)/shard_map/all_to_all | solution.py:69
  102.3 3.5 %all_to_all.38 = bf16[4,88,2048]{2,1,0:T(8,128)(2,1)} reshape(bf16[4,88,16,128]{3,2,1,0:T(8,128)(2,1)} %copy.52) | data formatting | bytes 2883584 | tf_op jit(solution)/shard_map/all_to_all | solution.py:69
  105.8 16.3 %all-to-all-done.1 = bf16[8,128,1408]{1,0,2:T(8,128)(2,1)S(1)} async-done(((bf16[8,128,1408]{1,0,2:T(8,128)(2,1)}), bf16[8,128,1408]{1,0,2:T(8,128)(2,1)S(1)}, u32[]{:S(2)}, u32[]{:S(2)}) %all-to-all-start.1) | async-done | bytes 2883616 | tf_op jit(solution)/shard_map/all_to_all | solution.py:30
  122.0 0.4 copy.47
  122.4 0.2 slice_bitcast_fusion
  122.6 1.5 %copy.64 = bf16[4,16,11,8,128]{4,3,1,2,0:T(8,128)(2,1)} copy(bf16[4,16,11,8,128]{4,3,2,1,0:T(8,128)(2,1)S(1)} %get-tuple-element.7) | data formatting | bytes 2883584 | tf_op jit(solution)/shard_map/slice | solution.py:35
  124.1 1.5 %copy.65 = bf16[4,16,11,8,128]{4,3,1,2,0:T(8,128)(2,1)} copy(bf16[4,16,11,8,128]{4,3,2,1,0:T(8,128)(2,1)S(1)} %get-tuple-element.8) | data formatting | bytes 2883584 | tf_op jit(solution)/shard_map/slice | solution.py:35
  (9 shorter events, 0.1 us)
Async XLA Ops:
  0.6 2.7 %copy-start.1 = (f32[4,128,1408]{2,1,0:T(8,128)S(1)}, f32[4,128,1408]{2,1,0:T(8,128)}, u32[]{:S(2)}) copy-start(f32[4,128,1408]{2,1,0:T(8,128)} %param.6) | copy-start | bytes 8650756
  3.6 11.5 %copy-start = (f32[4,128,1408]{2,1,0:T(8,128)S(1)}, f32[4,128,1408]{2,1,0:T(8,128)}, u32[]{:S(2)}) copy-start(f32[4,128,1408]{2,1,0:T(8,128)} %param.5) | copy-start | bytes 8650756
  8.0 25.2 %all-to-all-start = ((f32[16,1,16896]{2,1,0:T(1,128)}), f32[16,1,16896]{2,1,0:T(1,128)}, u32[]{:S(2)}, u32[]{:S(2)}) async-start(f32[16,1,16896]{2,1,0:T(1,128)} %broadcast_in_dim.4), calls=%async_computation | async-start | bytes 2162688 | tf_op jit(solution)/shard_map/all_to_all | solution.py:11
  17.9 4.7 %copy-start.4 = (f32[128,4]{0,1:T(4,128)S(1)}, f32[128,4]{0,1:T(4,128)}, u32[]{:S(2)}) copy-start(f32[128,4]{0,1:T(4,128)} %param.8) | copy-start | bytes 6148
  17.9 4.7 %copy-start.5 = (f32[128]{0:T(128)S(1)}, f32[128]{0:T(128)}, u32[]{:S(2)}) copy-start(f32[128]{0:T(128)} %param.9) | copy-start | bytes 1540
  17.9 22.5 %copy-start.2 = (f32[4,1408,128]{2,1,0:T(8,128)S(1)}, f32[4,1408,128]{2,1,0:T(8,128)}, u32[]{:S(2)}) copy-start(f32[4,1408,128]{2,1,0:T(8,128)} %param.7) | copy-start | bytes 8650756
  33.8 16.7 %all-to-all-start.3 = ((bf16[16,128,4]{1,2,0:T(4,128)(2,1)}), bf16[16,128,4]{1,2,0:T(4,128)(2,1)S(1)}, u32[]{:S(2)}, u32[]{:S(2)}) async-start(bf16[16,128,4]{1,2,0:T(4,128)(2,1)} %broadcast_in_dim.5), calls=%async_computation.3 | async-start | bytes 32768 | tf_op jit(solution)/shard_map/all_to_all | solution.py:11
  48.1 9.6 %copy-start.3 = (f32[4,128,1408]{1,0,2:T(4,128)S(1)}, f32[4,128,1408]{1,0,2:T(4,128)}, u32[]{:S(2)}) copy-start(f32[4,128,1408]{1,0,2:T(4,128)} %copy.44) | copy-start | bytes 8650756
  50.5 28.4 %all-to-all-start.2 = ((bf16[4,1408,128]{2,0,1:T(4,128)(2,1)}), bf16[4,1408,128]{2,0,1:T(4,128)(2,1)}, u32[]{:S(2)}, u32[]{:S(2)}) async-start(bf16[4,1408,128]{2,0,1:T(4,128)(2,1)} %fusion), calls=%async_computation.2 | async-start | bytes 2883584 | tf_op jit(solution)/shard_map/all_to_all | solution.py:69
  78.8 43.2 %all-to-all-start.1 = ((bf16[8,128,1408]{1,0,2:T(8,128)(2,1)}), bf16[8,128,1408]{1,0,2:T(8,128)(2,1)S(1)}, u32[]{:S(2)}, u32[]{:S(2)}) async-start(bf16[8,128,1408]{1,0,2:T(8,128)(2,1)} %pad_maximum_fusion), calls=%async_computation.1 | async-start | bytes 5767168 | tf_op jit(solution)/shard_map/all_to_all | solution.py:30
where the time goes:
time: 126 us
  waiting for transfers between devices  38.8 us (31%)
  local copies, waits for them, and re-layouts  25.8 us (20%)
  other arithmetic  24.1 us (19%)
  starting transfers between devices  21.5 us (17%)
  blocking collectives  14.6 us (12%)
    all_to_all x1, waiting for transfers between devices, side_by_side(): lax.all_to_all(both, axis, split_axis=split_dim, concat_axis=concat_dim,...  16.3 us
    all_gather x1, blocking collectives, local(): serve_router = lax.all_gather(row_router, 'bank', axis=1, tiled=True)  14.6 us
    all_to_all x1, waiting for transfers between devices, local(): lax.all_to_all(narrow_down, 'zero', split_axis=1, concat_axis=2, tiled=True)  12 us
    all_to_all x2, waiting for transfers between devices, copy_for_each(): lax.all_to_all(jnp.broadcast_to(x[None], (count, *x.shape)), axis, 0, 0,...  10.6 us
    all_to_all x2, starting transfers between devices, copy_for_each(): lax.all_to_all(jnp.broadcast_to(x[None], (count, *x.shape)), axis, 0, 0,...  10.6 us
    unnamed x16, local copies, waits for them, and re-layouts  8.94 us
    convert_element_type x1, other arithmetic, local(): (master_down / jnp.expand_dims(scale_down, 2)).astype(jnp.bfloat16)  7.73 us
    all_to_all x1, starting transfers between devices, local(): lax.all_to_all(narrow_down, 'zero', split_axis=1, concat_axis=2, tiled=True)  7.2 us
  transfers between devices with their start and end apart: 4, of which 3 were waited for; matrix products, arithmetic and copies ran while one was open for 28% of the time, Pallas kernels for 0%

commit v1 on v0

--- a/solution.py
+++ b/solution.py
@@ -66,7 +66,9 @@
         (master_down / jnp.expand_dims(scale_down, 2)).astype(jnp.bfloat16),
     )
     final_gate, final_up = side_by_side((narrow_gate, narrow_up), "zero", 2, 1, 0)
-    final_down = lax.all_to_all(narrow_down, "zero", split_axis=1, concat_axis=2, tiled=True)
+    parts = jnp.split(narrow_down, lax.axis_size("zero"), axis=1)
+    incoming = lax.all_to_all(jnp.stack(parts), "zero", 0, 0)
+    final_down = jnp.concatenate(incoming, axis=2)
     scale_gate = lax.dynamic_slice_in_dim(
         scale_gate, lax.axis_index("zero") * final_gate.shape[2], final_gate.shape[2], axis=1
     )

time: 126 us -> 119 us (0.944)
  other arithmetic: 24.1 us -> 17.1 us
  waiting for transfers between devices: 38.8 us -> 43.5 us
  local copies, waits for them, and re-layouts: 25.8 us -> 21.7 us
    convert_element_type x1, other arithmetic: 7.73 us -> 0.94 us  [local(): (master_down / jnp.expand_dims(scale_down, 2)).astype(jnp.bfloat16)]
    all_to_all x2 -> x0, local copies, waits for them, and re-layouts: 6.5 us -> none  [local(): lax.all_to_all(narrow_down, 'zero', split_axis=1, concat_axis=2, tiled=True)]
    all_to_all x1, waiting for transfers between devices: 16.3 us -> 20.1 us  [side_by_side(): lax.all_to_all(both, axis, split_axis=split_dim, concat_axis=concat_dim,...]
    reshape x0 -> x1, local copies, waits for them, and re-layouts: none -> 2.65 us  [local(): final_down = jnp.concatenate(incoming, axis=2)]
    unnamed x16 -> x31, local copies, waits for them, and re-layouts: 8.94 us -> 9.83 us
  transfers between devices with their start and end apart: 4 -> 4, of which waited for: 3 -> 4; matrix products, arithmetic and copies ran while one was open for 28% -> 23% of each run, Pallas kernels for 0% -> 0%
where the time goes in v1:
time: 119 us
  waiting for transfers between devices  43.5 us (37%)
  local copies, waits for them, and re-layouts  21.7 us (18%)
  starting transfers between devices  20.9 us (18%)
  other arithmetic  17.1 us (14%)
  blocking collectives  14.6 us (12%)
    all_to_all x1, waiting for transfers between devices, side_by_side(): lax.all_to_all(both, axis, split_axis=split_dim, concat_axis=concat_dim,...  20.1 us
    all_gather x1, blocking collectives, local(): serve_router = lax.all_gather(row_router, 'bank', axis=1, tiled=True)  14.6 us
    all_to_all x1, waiting for transfers between devices, local(): incoming = lax.all_to_all(jnp.stack(parts), 'zero', 0, 0)  12 us
    all_to_all x2, waiting for transfers between devices, copy_for_each(): lax.all_to_all(jnp.broadcast_to(x[None], (count, *x.shape)), axis, 0, 0,...  11.4 us
    all_to_all x2, starting transfers between devices, copy_for_each(): lax.all_to_all(jnp.broadcast_to(x[None], (count, *x.shape)), axis, 0, 0,...  10.6 us
    unnamed x31, local copies, waits for them, and re-layouts  9.83 us
    all_to_all x1, starting transfers between devices, local(): incoming = lax.all_to_all(jnp.stack(parts), 'zero', 0, 0)  6.64 us
    convert_element_type x1, other arithmetic, local(): (master_up / jnp.expand_dims(scale_up, 1)).astype(jnp.bfloat16)  6.53 us
  transfers between devices with their start and end apart: 4, of which 4 were waited for; matrix products, arithmetic and copies ran while one was open for 23% of the time, Pallas kernels for 0%

profile of v1, /device:TPU:224, one launch (start us, length us, event | category | flops | bytes accessed | tf_op | source)
XLA Modules:
  0.0 118.8 jit_solution(10859366820863062998)
XLA Ops:
  0.6 0.0 copy-start
  0.6 2.8 %abs_reduce_fusion = f32[4,1408]{1,0:T(4,128)S(1)} fusion(f32[4,1408,128]{2,1,0:T(8,128)} %param.7), kind=kLoop, calls=%fused_computation.2 | loop fusion | flops 1436160 | bytes 2906112 | tf_op jit(solution)/shard_map/reduce_sum | solution.py:56
  3.5 0.0 copy-done
  3.5 0.2 abs_reduce_fusion.1
  3.7 2.1 %abs_reduce_fusion.2 = f32[4,1408]{1,0:T(4,128)S(1)} fusion(f32[4,128,1408]{2,1,0:T(8,128)} %param.5), kind=kLoop, calls=%fused_computation.4 | loop fusion | flops 1436160 | bytes 2906112 | tf_op jit(solution)/shard_map/reduce_sum | solution.py:54
  5.8 1.5 %broadcast_in_dim.4 = f32[16,1,16896]{2,1,0:T(1,128)} broadcast(f32[16896]{0:T(1024)S(1)} %pad_maximum_fusion.1), dimensions={2} | broadcast | bytes 1148928 | tf_op jit(solution)/shard_map/broadcast_in_dim | solution.py:11
  7.4 7.1 %all-to-all-start = ((f32[16,1,16896]{2,1,0:T(1,128)}), f32[16,1,16896]{2,1,0:T(1,128)}, u32[]{:S(2)}, u32[]{:S(2)}) async-start(f32[16,1,16896]{2,1,0:T(1,128)} %broadcast_in_dim.4), calls=%async_computation | async-start | bytes 2162688 | tf_op jit(solution)/shard_map/all_to_all | solution.py:11
  14.5 2.8 %copy.42 = f32[4,128,1408]{1,0,2:T(4,128)} copy(f32[4,128,1408]{2,1,0:T(8,128)S(1)} %copy-done) | data formatting | bytes 5767168 | tf_op args[1]
  17.3 0.0 copy-start.4
  17.3 0.0 copy-start.5
  17.3 0.0 copy-start.1
  17.3 4.7 %copy.40 = f32[4,128,1408]{1,0,2:T(4,128)} copy(f32[4,128,1408]{2,1,0:T(8,128)} %param.5) | data formatting | bytes 5767168 | tf_op args[0]
  22.0 0.0 copy-done.4
  22.0 0.0 copy-done.5
  22.0 10.6 %all-to-all-done = f32[16,1,16896]{2,1,0:T(1,128)} async-done(((f32[16,1,16896]{2,1,0:T(1,128)}), f32[16,1,16896]{2,1,0:T(1,128)}, u32[]{:S(2)}, u32[]{:S(2)}) %all-to-all-start) | async-done | bytes 1081376 | tf_op jit(solution)/shard_map/all_to_all | solution.py:11
  32.6 0.6 broadcast_in_dim.5
  33.2 3.5 %all-to-all-start.3 = ((bf16[16,128,4]{1,2,0:T(4,128)(2,1)}), bf16[16,128,4]{1,2,0:T(4,128)(2,1)S(1)}, u32[]{:S(2)}, u32[]{:S(2)}) async-start(bf16[16,128,4]{1,2,0:T(4,128)(2,1)} %broadcast_in_dim.5), calls=%async_computation.3 | async-start | bytes 32768 | tf_op jit(solution)/shard_map/all_to_all | solution.py:11
  36.7 1.9 %reduce_sum.39 = f32[16896]{0:T(1024)S(1)} reduce(f32[16,1,16896]{2,1,0:T(1,128)} %all-to-all-done, f32[]{:T(128)} %constant.6.clone.1), dimensions={0,1}, to_apply=%region_3.0 | reduce | flops 253440 | bytes 1148932 | tf_op jit(solution)/shard_map/reduce_sum | solution.py:15
  38.6 0.0 copy-done.1
  38.7 0.9 divide_convert_fusion
  40.0 0.0 copy-start.3
  40.0 1.1 copy-done.3
  41.1 1.2 copy.41
  42.2 1.2 copy.39
  43.4 0.0 copy-start.2
  43.4 0.8 all-to-all-done.3
  44.2 6.6 %all-to-all-start.2 = ((bf16[16,4,88,128]{3,2,1,0:T(8,128)(2,1)}), bf16[16,4,88,128]{3,2,1,0:T(8,128)(2,1)}, u32[]{:S(2)}, u32[]{:S(2)}) async-start(bf16[16,4,88,128]{3,2,1,0:T(8,128)(2,1)} %copy-done.3), calls=%async_computation.2 | async-start | bytes 2883584 | tf_op jit(solution)/shard_map/all_to_all | solution.py:70
  50.9 0.0 copy-done.2
  50.9 6.5 %divide_convert_fusion.1 = (bf16[4,128,1408]{1,0,2:T(4,128)(2,1)S(1)}, bf16[4,128,1408]{1,0,2:T(4,128)(2,1)S(1)}) fusion(f32[4,128,1408]{1,0,2:T(4,128)S(1)} %copy-done.2, f32[4,1408]{0,1:T(8,128)} %copy.41, f32[4,128,1408]{1,0,2:T(4,128)} %copy.40, f32[4,1408]{0,1:T(8,128)} %copy.39), kind=kLoop, calls=%fused_computation.5 | loop fusion | flops 2883584 | bytes 8695808 | tf_op jit(solution)/shard_map/convert_element_type | solution.py:65
  57.4 2.6 %pad_maximum_fusion = bf16[8,128,1408]{1,0,2:T(8,128)(2,1)} fusion(bf16[4,128,1408]{1,0,2:T(4,128)(2,1)S(1)} %get-tuple-element.12, bf16[4,128,1408]{1,0,2:T(4,128)(2,1)S(1)} %get-tuple-element.13), kind=kLoop, calls=%fused_computation | loop fusion | flops 5767168 | bytes 5767168 | tf_op jit(solution)/shard_map/concatenate | solution.py:28
  60.0 12.0 %all-to-all-done.2 = bf16[16,4,88,128]{3,2,1,0:T(8,128)(2,1)} async-done(((bf16[16,4,88,128]{3,2,1,0:T(8,128)(2,1)}), bf16[16,4,88,128]{3,2,1,0:T(8,128)(2,1)}, u32[]{:S(2)}, u32[]{:S(2)}) %all-to-all-start.2) | async-done | bytes 1441824 | tf_op jit(solution)/shard_map/all_to_all | solution.py:70
  72.0 3.7 %all-to-all-start.1 = ((bf16[8,128,1408]{1,0,2:T(8,128)(2,1)}), bf16[8,128,1408]{1,0,2:T(8,128)(2,1)S(1)}, u32[]{:S(2)}, u32[]{:S(2)}) async-start(bf16[8,128,1408]{1,0,2:T(8,128)(2,1)} %pad_maximum_fusion), calls=%async_computation.1 | async-start | bytes 5767168 | tf_op jit(solution)/shard_map/all_to_all | solution.py:30
  75.8 14.6 %all-gather = bf16[16,4,2048]{2,1,0:T(4,128)(2,1)S(1)} all-gather(bf16[1,4,2048]{2,1,0:T(4,128)(2,1)S(1)} %bitcast.93), channel_id=1, replica_groups=mesh['bank'=16,'zero'=16] {'bank'}, dimensions={0}, use_global_device_ids=true | all-gather | bytes 278528 | tf_op jit(solution)/shard_map/all_gather | solution.py:83
  90.4 0.8 reshape.85
  91.2 0.6 constant_dynamic-slice_fusion.2
  91.8 0.7 constant_dynamic-slice_fusion
  92.5 2.6 %copy_bitcast_fusion = bf16[4,88,2048]{2,1,0:T(8,128)(2,1)} fusion(bf16[16,4,88,128]{3,2,1,0:T(8,128)(2,1)} %all-to-all-done.2), kind=kLoop, calls=%fused_computation.7 | loop fusion | bytes 2883584 | tf_op jit(solution)/shard_map/reshape | solution.py:71
  95.1 20.1 %all-to-all-done.1 = bf16[8,128,1408]{1,0,2:T(8,128)(2,1)S(1)} async-done(((bf16[8,128,1408]{1,0,2:T(8,128)(2,1)}), bf16[8,128,1408]{1,0,2:T(8,128)(2,1)S(1)}, u32[]{:S(2)}, u32[]{:S(2)}) %all-to-all-start.1) | async-done | bytes 2883616 | tf_op jit(solution)/shard_map/all_to_all | solution.py:30
  115.2 0.4 copy.43
  115.6 0.2 slice_bitcast_fusion
  115.8 1.5 %copy.58 = bf16[4,16,11,8,128]{4,3,1,2,0:T(8,128)(2,1)} copy(bf16[4,16,11,8,128]{4,3,2,1,0:T(8,128)(2,1)S(1)} %get-tuple-element.8) | data formatting | bytes 2883584 | tf_op jit(solution)/shard_map/slice | solution.py:35
  117.3 1.5 %copy.57 = bf16[4,16,11,8,128]{4,3,1,2,0:T(8,128)(2,1)} copy(bf16[4,16,11,8,128]{4,3,2,1,0:T(8,128)(2,1)S(1)} %get-tuple-element.7) | data formatting | bytes 2883584 | tf_op jit(solution)/shard_map/slice | solution.py:35
  (25 shorter events, 0.4 us)
Async XLA Ops:
  0.6 2.8 %copy-start = (f32[4,128,1408]{2,1,0:T(8,128)S(1)}, f32[4,128,1408]{2,1,0:T(8,128)}, u32[]{:S(2)}) copy-start(f32[4,128,1408]{2,1,0:T(8,128)} %param.6) | copy-start | bytes 8650756
  7.4 25.2 %all-to-all-start = ((f32[16,1,16896]{2,1,0:T(1,128)}), f32[16,1,16896]{2,1,0:T(1,128)}, u32[]{:S(2)}, u32[]{:S(2)}) async-start(f32[16,1,16896]{2,1,0:T(1,128)} %broadcast_in_dim.4), calls=%async_computation | async-start | bytes 2162688 | tf_op jit(solution)/shard_map/all_to_all | solution.py:11
  17.3 4.7 %copy-start.4 = (f32[128,4]{0,1:T(4,128)S(1)}, f32[128,4]{0,1:T(4,128)}, u32[]{:S(2)}) copy-start(f32[128,4]{0,1:T(4,128)} %param.8) | copy-start | bytes 6148
  17.3 4.7 %copy-start.5 = (f32[128]{0:T(128)S(1)}, f32[128]{0:T(128)}, u32[]{:S(2)}) copy-start(f32[128]{0:T(128)} %param.9) | copy-start | bytes 1540
  17.3 21.3 %copy-start.1 = (f32[4,1408,128]{2,1,0:T(8,128)S(1)}, f32[4,1408,128]{2,1,0:T(8,128)}, u32[]{:S(2)}) copy-start(f32[4,1408,128]{2,1,0:T(8,128)} %param.7) | copy-start | bytes 8650756
  33.2 11.0 %all-to-all-start.3 = ((bf16[16,128,4]{1,2,0:T(4,128)(2,1)}), bf16[16,128,4]{1,2,0:T(4,128)(2,1)S(1)}, u32[]{:S(2)}, u32[]{:S(2)}) async-start(bf16[16,128,4]{1,2,0:T(4,128)(2,1)} %broadcast_in_dim.5), calls=%async_computation.3 | async-start | bytes 32768 | tf_op jit(solution)/shard_map/all_to_all | solution.py:11
  40.0 1.1 copy-start.3
  43.4 7.5 %copy-start.2 = (f32[4,128,1408]{1,0,2:T(4,128)S(1)}, f32[4,128,1408]{1,0,2:T(4,128)}, u32[]{:S(2)}) copy-start(f32[4,128,1408]{1,0,2:T(4,128)} %copy.42) | copy-start | bytes 8650756
  44.2 27.8 %all-to-all-start.2 = ((bf16[16,4,88,128]{3,2,1,0:T(8,128)(2,1)}), bf16[16,4,88,128]{3,2,1,0:T(8,128)(2,1)}, u32[]{:S(2)}, u32[]{:S(2)}) async-start(bf16[16,4,88,128]{3,2,1,0:T(8,128)(2,1)} %copy-done.3), calls=%async_computation.2 | async-start | bytes 2883584 | tf_op jit(solution)/shard_map/all_to_all | solution.py:70
  72.0 43.2 %all-to-all-start.1 = ((bf16[8,128,1408]{1,0,2:T(8,128)(2,1)}), bf16[8,128,1408]{1,0,2:T(8,128)(2,1)S(1)}, u32[]{:S(2)}, u32[]{:S(2)}) async-start(bf16[8,128,1408]{1,0,2:T(8,128)(2,1)} %pad_maximum_fusion), calls=%async_computation.1 | async-start | bytes 5767168 | tf_op jit(solution)/shard_map/all_to_all | solution.py:30
